TPU v7x, 32 devices: a 4x2x2 block of a 4x4x8 slice. The times are simulated.
32 devices in a mesh: data: 4 (over y, z), model: 8 (over x, core).
Axes of the slice: x: 4, y: 2, z: 2, core: 2. Of those that a mesh axis runs over, the one named last changes fastest.
The devices are a block of a 4x4x8 slice.
Arguments:
- x: bfloat16 [768, 16, 1024], P('data'), parts along dimension 0
- w_in: bfloat16 [1024, 4, 8192], P(None, None, 'model')
- w_rec: bfloat16 [8192, 4, 8192], P(None, None, 'model')
- gate_bias: float32 [4, 8192], P(None, 'model')
- h_init: float32 [768, 8192], P('data', 'model'), parts along dimension 0
- c_init: float32 [768, 8192], P('data', 'model'), parts along dimension 0
Outputs:
- output 1: bfloat16 [768, 16, 8192], P('data', None, 'model'), parts along dimension 0
- output 2: float32 [768, 8192], P('data', 'model'), parts along dimension 0
- output 3: float32 [768, 8192], P('data', 'model'), parts along dimension 0
There are 4 independent parts. A program takes and returns all parts, laid end to end along the dimension named above; an argument that names none is the same for every part.
All inputs are finite; a program needn't handle non-finite values.
Results may differ from a plain program's by a relative error of at most 0.00305013.
Values are sent between devices in bfloat16 or wider.
A program may use at most 768 MiB of HBM per device.

v0:
```python
import jax
import jax.numpy as jnp
from jax import lax
from jax.sharding import PartitionSpec as P


def solution(mesh):
    def local_fn(x, w_in, w_rec, gate_bias, h_init, c_init):
        in_dim = w_in.shape[0]
        hidden = w_rec.shape[0]
        local_units = w_rec.shape[2]
        batch_rows = x.shape[0]
        w_in_flat = w_in.reshape(in_dim, 4 * local_units)
        w_rec_flat = w_rec.reshape(hidden, 4 * local_units)

        def step_fn(carry_in, x_step):
            h_prev, c_prev = carry_in
            h_gathered = lax.all_gather(h_prev.astype(jnp.bfloat16), "model", axis=1, tiled=True)
            gate_pre = jnp.dot(x_step, w_in_flat, preferred_element_type=jnp.float32) + jnp.dot(
                h_gathered, w_rec_flat, preferred_element_type=jnp.float32)
            gate_pre = gate_pre.reshape(batch_rows, 4, local_units) + gate_bias
            c_next = jax.nn.sigmoid(gate_pre[:, 1]) * c_prev + jax.nn.sigmoid(gate_pre[:, 0]) * jnp.tanh(gate_pre[:, 3])
            h_next = jax.nn.sigmoid(gate_pre[:, 2]) * jnp.tanh(c_next)
            return (h_next, c_next), h_next.astype(jnp.bfloat16)

        (h_last, c_last), y_steps = lax.scan(step_fn, (h_init, c_init), jnp.swapaxes(x, 0, 1))
        return jnp.swapaxes(y_steps, 0, 1), h_last, c_last

    return jax.shard_map(
        local_fn,
        mesh=mesh,
        in_specs=(P("data", None, None), P(None, None, "model"), P(None, None, "model"),
                  P(None, "model"), P("data", "model"), P("data", "model")),
        out_specs=(P("data", None, "model"), P("data", "model"), P("data", "model")),
        check_vma=False,
    )
```

profile of v0, /device:TPU:81, one launch (start us, length us, event | category | flops | bytes accessed | tf_op | source)
XLA Modules:
  0.0 1026.1 jit_solution(9261776827997799819)
XLA Ops:
  7.2 2.1 copy.39
  9.3 44.1 %copy.14 = bf16[1024,8,4,1024]{3,1,2,0:T(8,128)(2,1)} copy(bf16[1024,8,4,1024]{3,2,1,0:T(4,128)(2,1)} %bitcast.11) | data formatting | bytes 134217728
  53.4 12.1 %copy.13 = bf16[128,8,4,1024]{3,1,2,0:T(8,128)(2,1)} copy(bf16[128,8,4,1024]{3,2,1,0:T(4,128)(2,1)} %bitcast.55) | data formatting | bytes 16777216
  65.5 9.1 copy.19
  74.6 935.7 %while.14 = (s32[]{:T(128)}, f32[192,1024]{1,0:T(8,128)S(1)}, f32[192,1024]{1,0:T(8,128)}, bf16[16,192,1024]{2,1,0:T(8,128)(2,1)}, bf16[16,192,1024]{2,1,0:T(8,1...) while((s32[]{:T(128)}, f32[192,1024]{1,0:T(8,128)S(1)}, ...), condition=%wide.region_1.2_spmd, body=%wide.region_0.1_spmd.sunk | while | flops 14500036608 | bytes 118767816 | solution.py:26
  75.5 7.0 fusion.34
  82.6 24.0 %all-gather.2.cloned.1.call-done = bf16[192,8192]{1,0:T(8,128)(2,1)} async-done(((bf16[192,1024]{1,0:T(8,128)(2,1)}), bf16[192,8192]{1,0:T(8,128)(2,1)}) %all-gather.2.cloned.1.call-update) | async-done | bytes 3145744 | tf_op jit(solution)/shard_map/while/body/eval_jaxpr/all_gather | solution.py:18
  106.6 27.2 %convolution_add_fusion.2 = f32[192,4096]{1,0:T(8,128)S(1)} fusion(f32[192,4096]{1,0:T(8,128)} %fusion.34, bf16[192,8192]{1,0:T(8,128)(2,1)} %all-gather.2.cloned.1.call-done, bf16[8192,4096]{1,0:T(8,128)(2,1)} %get-tuple-element.148), kind=kOutput, calls=%fused_computation.clone.1 | convolution fusion | flops 12885688320 | bytes 76546048 | tf_op jit(solution)/shard_map/while/body/eval_jaxpr/dot_general | solution.py:19
  135.0 1.6 bitcast_dynamic-update-slice_fusion.2
  138.3 7.0 fusion.34
  145.3 19.6 %all-gather.2.cloned.1.call-done = bf16[192,8192]{1,0:T(8,128)(2,1)} async-done(((bf16[192,1024]{1,0:T(8,128)(2,1)}), bf16[192,8192]{1,0:T(8,128)(2,1)}) %all-gather.2.cloned.1.call-update) | async-done | bytes 3145744 | tf_op jit(solution)/shard_map/while/body/eval_jaxpr/all_gather | solution.py:18
  164.9 27.2 %convolution_add_fusion.2 = f32[192,4096]{1,0:T(8,128)S(1)} fusion(f32[192,4096]{1,0:T(8,128)} %fusion.34, bf16[192,8192]{1,0:T(8,128)(2,1)} %all-gather.2.cloned.1.call-done, bf16[8192,4096]{1,0:T(8,128)(2,1)} %get-tuple-element.148), kind=kOutput, calls=%fused_computation.clone.1 | convolution fusion | flops 12885688320 | bytes 76546048 | tf_op jit(solution)/shard_map/while/body/eval_jaxpr/dot_general | solution.py:19
  193.3 1.6 bitcast_dynamic-update-slice_fusion.2
  196.7 7.0 fusion.34
  203.7 19.6 %all-gather.2.cloned.1.call-done = bf16[192,8192]{1,0:T(8,128)(2,1)} async-done(((bf16[192,1024]{1,0:T(8,128)(2,1)}), bf16[192,8192]{1,0:T(8,128)(2,1)}) %all-gather.2.cloned.1.call-update) | async-done | bytes 3145744 | tf_op jit(solution)/shard_map/while/body/eval_jaxpr/all_gather | solution.py:18
  223.3 27.2 %convolution_add_fusion.2 = f32[192,4096]{1,0:T(8,128)S(1)} fusion(f32[192,4096]{1,0:T(8,128)} %fusion.34, bf16[192,8192]{1,0:T(8,128)(2,1)} %all-gather.2.cloned.1.call-done, bf16[8192,4096]{1,0:T(8,128)(2,1)} %get-tuple-element.148), kind=kOutput, calls=%fused_computation.clone.1 | convolution fusion | flops 12885688320 | bytes 76546048 | tf_op jit(solution)/shard_map/while/body/eval_jaxpr/dot_general | solution.py:19
  255.1 7.0 fusion.34
  262.1 19.3 %all-gather.2.cloned.1.call-done = bf16[192,8192]{1,0:T(8,128)(2,1)} async-done(((bf16[192,1024]{1,0:T(8,128)(2,1)}), bf16[192,8192]{1,0:T(8,128)(2,1)}) %all-gather.2.cloned.1.call-update) | async-done | bytes 3145744 | tf_op jit(solution)/shard_map/while/body/eval_jaxpr/all_gather | solution.py:18
  281.4 27.2 %convolution_add_fusion.2 = f32[192,4096]{1,0:T(8,128)S(1)} fusion(f32[192,4096]{1,0:T(8,128)} %fusion.34, bf16[192,8192]{1,0:T(8,128)(2,1)} %all-gather.2.cloned.1.call-done, bf16[8192,4096]{1,0:T(8,128)(2,1)} %get-tuple-element.148), kind=kOutput, calls=%fused_computation.clone.1 | convolution fusion | flops 12885688320 | bytes 76546048 | tf_op jit(solution)/shard_map/while/body/eval_jaxpr/dot_general | solution.py:19
  309.8 1.6 bitcast_dynamic-update-slice_fusion.2
  313.1 7.0 fusion.34
  320.1 19.3 %all-gather.2.cloned.1.call-done = bf16[192,8192]{1,0:T(8,128)(2,1)} async-done(((bf16[192,1024]{1,0:T(8,128)(2,1)}), bf16[192,8192]{1,0:T(8,128)(2,1)}) %all-gather.2.cloned.1.call-update) | async-done | bytes 3145744 | tf_op jit(solution)/shard_map/while/body/eval_jaxpr/all_gather | solution.py:18
  339.4 27.2 %convolution_add_fusion.2 = f32[192,4096]{1,0:T(8,128)S(1)} fusion(f32[192,4096]{1,0:T(8,128)} %fusion.34, bf16[192,8192]{1,0:T(8,128)(2,1)} %all-gather.2.cloned.1.call-done, bf16[8192,4096]{1,0:T(8,128)(2,1)} %get-tuple-element.148), kind=kOutput, calls=%fused_computation.clone.1 | convolution fusion | flops 12885688320 | bytes 76546048 | tf_op jit(solution)/shard_map/while/body/eval_jaxpr/dot_general | solution.py:19
  371.1 7.0 fusion.34
  378.2 19.3 %all-gather.2.cloned.1.call-done = bf16[192,8192]{1,0:T(8,128)(2,1)} async-done(((bf16[192,1024]{1,0:T(8,128)(2,1)}), bf16[192,8192]{1,0:T(8,128)(2,1)}) %all-gather.2.cloned.1.call-update) | async-done | bytes 3145744 | tf_op jit(solution)/shard_map/while/body/eval_jaxpr/all_gather | solution.py:18
  397.5 27.2 %convolution_add_fusion.2 = f32[192,4096]{1,0:T(8,128)S(1)} fusion(f32[192,4096]{1,0:T(8,128)} %fusion.34, bf16[192,8192]{1,0:T(8,128)(2,1)} %all-gather.2.cloned.1.call-done, bf16[8192,4096]{1,0:T(8,128)(2,1)} %get-tuple-element.148), kind=kOutput, calls=%fused_computation.clone.1 | convolution fusion | flops 12885688320 | bytes 76546048 | tf_op jit(solution)/shard_map/while/body/eval_jaxpr/dot_general | solution.py:19
  425.8 1.6 bitcast_dynamic-update-slice_fusion.2
  429.2 7.0 fusion.34
  436.2 19.6 %all-gather.2.cloned.1.call-done = bf16[192,8192]{1,0:T(8,128)(2,1)} async-done(((bf16[192,1024]{1,0:T(8,128)(2,1)}), bf16[192,8192]{1,0:T(8,128)(2,1)}) %all-gather.2.cloned.1.call-update) | async-done | bytes 3145744 | tf_op jit(solution)/shard_map/while/body/eval_jaxpr/all_gather | solution.py:18
  455.8 27.2 %convolution_add_fusion.2 = f32[192,4096]{1,0:T(8,128)S(1)} fusion(f32[192,4096]{1,0:T(8,128)} %fusion.34, bf16[192,8192]{1,0:T(8,128)(2,1)} %all-gather.2.cloned.1.call-done, bf16[8192,4096]{1,0:T(8,128)(2,1)} %get-tuple-element.148), kind=kOutput, calls=%fused_computation.clone.1 | convolution fusion | flops 12885688320 | bytes 76546048 | tf_op jit(solution)/shard_map/while/body/eval_jaxpr/dot_general | solution.py:19
  484.2 1.6 bitcast_dynamic-update-slice_fusion.2
  487.6 7.0 fusion.34
  494.6 19.6 %all-gather.2.cloned.1.call-done = bf16[192,8192]{1,0:T(8,128)(2,1)} async-done(((bf16[192,1024]{1,0:T(8,128)(2,1)}), bf16[192,8192]{1,0:T(8,128)(2,1)}) %all-gather.2.cloned.1.call-update) | async-done | bytes 3145744 | tf_op jit(solution)/shard_map/while/body/eval_jaxpr/all_gather | solution.py:18
  514.2 27.2 %convolution_add_fusion.2 = f32[192,4096]{1,0:T(8,128)S(1)} fusion(f32[192,4096]{1,0:T(8,128)} %fusion.34, bf16[192,8192]{1,0:T(8,128)(2,1)} %all-gather.2.cloned.1.call-done, bf16[8192,4096]{1,0:T(8,128)(2,1)} %get-tuple-element.148), kind=kOutput, calls=%fused_computation.clone.1 | convolution fusion | flops 12885688320 | bytes 76546048 | tf_op jit(solution)/shard_map/while/body/eval_jaxpr/dot_general | solution.py:19
  542.6 1.6 bitcast_dynamic-update-slice_fusion.2
  545.9 7.0 fusion.34
  553.0 19.6 %all-gather.2.cloned.1.call-done = bf16[192,8192]{1,0:T(8,128)(2,1)} async-done(((bf16[192,1024]{1,0:T(8,128)(2,1)}), bf16[192,8192]{1,0:T(8,128)(2,1)}) %all-gather.2.cloned.1.call-update) | async-done | bytes 3145744 | tf_op jit(solution)/shard_map/while/body/eval_jaxpr/all_gather | solution.py:18
  572.5 27.2 %convolution_add_fusion.2 = f32[192,4096]{1,0:T(8,128)S(1)} fusion(f32[192,4096]{1,0:T(8,128)} %fusion.34, bf16[192,8192]{1,0:T(8,128)(2,1)} %all-gather.2.cloned.1.call-done, bf16[8192,4096]{1,0:T(8,128)(2,1)} %get-tuple-element.148), kind=kOutput, calls=%fused_computation.clone.1 | convolution fusion | flops 12885688320 | bytes 76546048 | tf_op jit(solution)/shard_map/while/body/eval_jaxpr/dot_general | solution.py:19
  604.3 7.0 fusion.34
  611.3 19.3 %all-gather.2.cloned.1.call-done = bf16[192,8192]{1,0:T(8,128)(2,1)} async-done(((bf16[192,1024]{1,0:T(8,128)(2,1)}), bf16[192,8192]{1,0:T(8,128)(2,1)}) %all-gather.2.cloned.1.call-update) | async-done | bytes 3145744 | tf_op jit(solution)/shard_map/while/body/eval_jaxpr/all_gather | solution.py:18
  630.6 27.2 %convolution_add_fusion.2 = f32[192,4096]{1,0:T(8,128)S(1)} fusion(f32[192,4096]{1,0:T(8,128)} %fusion.34, bf16[192,8192]{1,0:T(8,128)(2,1)} %all-gather.2.cloned.1.call-done, bf16[8192,4096]{1,0:T(8,128)(2,1)} %get-tuple-element.148), kind=kOutput, calls=%fused_computation.clone.1 | convolution fusion | flops 12885688320 | bytes 76546048 | tf_op jit(solution)/shard_map/while/body/eval_jaxpr/dot_general | solution.py:19
  662.3 7.0 fusion.34
  669.3 19.6 %all-gather.2.cloned.1.call-done = bf16[192,8192]{1,0:T(8,128)(2,1)} async-done(((bf16[192,1024]{1,0:T(8,128)(2,1)}), bf16[192,8192]{1,0:T(8,128)(2,1)}) %all-gather.2.cloned.1.call-update) | async-done | bytes 3145744 | tf_op jit(solution)/shard_map/while/body/eval_jaxpr/all_gather | solution.py:18
  688.9 27.2 %convolution_add_fusion.2 = f32[192,4096]{1,0:T(8,128)S(1)} fusion(f32[192,4096]{1,0:T(8,128)} %fusion.34, bf16[192,8192]{1,0:T(8,128)(2,1)} %all-gather.2.cloned.1.call-done, bf16[8192,4096]{1,0:T(8,128)(2,1)} %get-tuple-element.148), kind=kOutput, calls=%fused_computation.clone.1 | convolution fusion | flops 12885688320 | bytes 76546048 | tf_op jit(solution)/shard_map/while/body/eval_jaxpr/dot_general | solution.py:19
  717.3 1.6 bitcast_dynamic-update-slice_fusion.2
  720.7 7.0 fusion.34
  727.7 19.3 %all-gather.2.cloned.1.call-done = bf16[192,8192]{1,0:T(8,128)(2,1)} async-done(((bf16[192,1024]{1,0:T(8,128)(2,1)}), bf16[192,8192]{1,0:T(8,128)(2,1)}) %all-gather.2.cloned.1.call-update) | async-done | bytes 3145744 | tf_op jit(solution)/shard_map/while/body/eval_jaxpr/all_gather | solution.py:18
  747.0 27.3 %convolution_add_fusion.2 = f32[192,4096]{1,0:T(8,128)S(1)} fusion(f32[192,4096]{1,0:T(8,128)} %fusion.34, bf16[192,8192]{1,0:T(8,128)(2,1)} %all-gather.2.cloned.1.call-done, bf16[8192,4096]{1,0:T(8,128)(2,1)} %get-tuple-element.148), kind=kOutput, calls=%fused_computation.clone.1 | convolution fusion | flops 12885688320 | bytes 76546048 | tf_op jit(solution)/shard_map/while/body/eval_jaxpr/dot_general | solution.py:19
  775.4 1.6 bitcast_dynamic-update-slice_fusion.2
  778.7 7.0 fusion.34
  785.7 19.6 %all-gather.2.cloned.1.call-done = bf16[192,8192]{1,0:T(8,128)(2,1)} async-done(((bf16[192,1024]{1,0:T(8,128)(2,1)}), bf16[192,8192]{1,0:T(8,128)(2,1)}) %all-gather.2.cloned.1.call-update) | async-done | bytes 3145744 | tf_op jit(solution)/shard_map/while/body/eval_jaxpr/all_gather | solution.py:18
  805.3 27.2 %convolution_add_fusion.2 = f32[192,4096]{1,0:T(8,128)S(1)} fusion(f32[192,4096]{1,0:T(8,128)} %fusion.34, bf16[192,8192]{1,0:T(8,128)(2,1)} %all-gather.2.cloned.1.call-done, bf16[8192,4096]{1,0:T(8,128)(2,1)} %get-tuple-element.148), kind=kOutput, calls=%fused_computation.clone.1 | convolution fusion | flops 12885688320 | bytes 76546048 | tf_op jit(solution)/shard_map/while/body/eval_jaxpr/dot_general | solution.py:19
  833.7 1.6 bitcast_dynamic-update-slice_fusion.2
  837.1 7.0 fusion.34
  844.1 19.3 %all-gather.2.cloned.1.call-done = bf16[192,8192]{1,0:T(8,128)(2,1)} async-done(((bf16[192,1024]{1,0:T(8,128)(2,1)}), bf16[192,8192]{1,0:T(8,128)(2,1)}) %all-gather.2.cloned.1.call-update) | async-done | bytes 3145744 | tf_op jit(solution)/shard_map/while/body/eval_jaxpr/all_gather | solution.py:18
  863.4 27.2 %convolution_add_fusion.2 = f32[192,4096]{1,0:T(8,128)S(1)} fusion(f32[192,4096]{1,0:T(8,128)} %fusion.34, bf16[192,8192]{1,0:T(8,128)(2,1)} %all-gather.2.cloned.1.call-done, bf16[8192,4096]{1,0:T(8,128)(2,1)} %get-tuple-element.148), kind=kOutput, calls=%fused_computation.clone.1 | convolution fusion | flops 12885688320 | bytes 76546048 | tf_op jit(solution)/shard_map/while/body/eval_jaxpr/dot_general | solution.py:19
  895.1 7.0 fusion.34
  902.1 19.3 %all-gather.2.cloned.1.call-done = bf16[192,8192]{1,0:T(8,128)(2,1)} async-done(((bf16[192,1024]{1,0:T(8,128)(2,1)}), bf16[192,8192]{1,0:T(8,128)(2,1)}) %all-gather.2.cloned.1.call-update) | async-done | bytes 3145744 | tf_op jit(solution)/shard_map/while/body/eval_jaxpr/all_gather | solution.py:18
  921.4 27.2 %convolution_add_fusion.2 = f32[192,4096]{1,0:T(8,128)S(1)} fusion(f32[192,4096]{1,0:T(8,128)} %fusion.34, bf16[192,8192]{1,0:T(8,128)(2,1)} %all-gather.2.cloned.1.call-done, bf16[8192,4096]{1,0:T(8,128)(2,1)} %get-tuple-element.148), kind=kOutput, calls=%fused_computation.clone.1 | convolution fusion | flops 12885688320 | bytes 76546048 | tf_op jit(solution)/shard_map/while/body/eval_jaxpr/dot_general | solution.py:19
  949.8 1.6 bitcast_dynamic-update-slice_fusion.2
  953.2 7.0 fusion.34
  960.2 19.3 %all-gather.2.cloned.1.call-done = bf16[192,8192]{1,0:T(8,128)(2,1)} async-done(((bf16[192,1024]{1,0:T(8,128)(2,1)}), bf16[192,8192]{1,0:T(8,128)(2,1)}) %all-gather.2.cloned.1.call-update) | async-done | bytes 3145744 | tf_op jit(solution)/shard_map/while/body/eval_jaxpr/all_gather | solution.py:18
  979.5 27.2 %convolution_add_fusion.2 = f32[192,4096]{1,0:T(8,128)S(1)} fusion(f32[192,4096]{1,0:T(8,128)} %fusion.34, bf16[192,8192]{1,0:T(8,128)(2,1)} %all-gather.2.cloned.1.call-done, bf16[8192,4096]{1,0:T(8,128)(2,1)} %get-tuple-element.148), kind=kOutput, calls=%fused_computation.clone.1 | convolution fusion | flops 12885688320 | bytes 76546048 | tf_op jit(solution)/shard_map/while/body/eval_jaxpr/dot_general | solution.py:19
  1010.3 9.3 copy.18
  (141 shorter events, 55.3 us)
Async XLA Ops:
  65.5 9.1 copy-start.3
  65.5 9.1 copy-start.4
  74.6 32.0 %all-gather.2.cloned.1.call-start = ((), (), s32[]{:S(2)}) async-start(), calls=%async_computation | async-start | bytes 3538944 | tf_op jit(solution)/shard_map/while/body/eval_jaxpr/all_gather | solution.py:18
  133.8 1.1 copy-start
  136.6 0.9 copy-start.1
  137.5 27.5 %all-gather.2.cloned.1.call-start = ((), (), s32[]{:S(2)}) async-start(), calls=%async_computation | async-start | bytes 3538944 | tf_op jit(solution)/shard_map/while/body/eval_jaxpr/all_gather | solution.py:18
  192.2 1.1 copy-start
  195.0 0.9 copy-start.1
  195.8 27.5 %all-gather.2.cloned.1.call-start = ((), (), s32[]{:S(2)}) async-start(), calls=%async_computation | async-start | bytes 3538944 | tf_op jit(solution)/shard_map/while/body/eval_jaxpr/all_gather | solution.py:18
  250.6 1.1 copy-start
  253.3 0.9 copy-start.1
  254.2 27.2 %all-gather.2.cloned.1.call-start = ((), (), s32[]{:S(2)}) async-start(), calls=%async_computation | async-start | bytes 3538944 | tf_op jit(solution)/shard_map/while/body/eval_jaxpr/all_gather | solution.py:18
  308.6 1.1 copy-start
  311.4 0.9 copy-start.1
  312.2 27.2 %all-gather.2.cloned.1.call-start = ((), (), s32[]{:S(2)}) async-start(), calls=%async_computation | async-start | bytes 3538944 | tf_op jit(solution)/shard_map/while/body/eval_jaxpr/all_gather | solution.py:18
  366.7 1.1 copy-start
  369.4 0.9 copy-start.1
  370.3 27.2 %all-gather.2.cloned.1.call-start = ((), (), s32[]{:S(2)}) async-start(), calls=%async_computation | async-start | bytes 3538944 | tf_op jit(solution)/shard_map/while/body/eval_jaxpr/all_gather | solution.py:18
  424.7 1.1 copy-start
  427.5 0.9 copy-start.1
  428.3 27.5 %all-gather.2.cloned.1.call-start = ((), (), s32[]{:S(2)}) async-start(), calls=%async_computation | async-start | bytes 3538944 | tf_op jit(solution)/shard_map/while/body/eval_jaxpr/all_gather | solution.py:18
  483.1 1.1 copy-start
  485.8 0.9 copy-start.1
  486.7 27.5 %all-gather.2.cloned.1.call-start = ((), (), s32[]{:S(2)}) async-start(), calls=%async_computation | async-start | bytes 3538944 | tf_op jit(solution)/shard_map/while/body/eval_jaxpr/all_gather | solution.py:18
  541.4 1.1 copy-start
  544.2 0.9 copy-start.1
  545.1 27.5 %all-gather.2.cloned.1.call-start = ((), (), s32[]{:S(2)}) async-start(), calls=%async_computation | async-start | bytes 3538944 | tf_op jit(solution)/shard_map/while/body/eval_jaxpr/all_gather | solution.py:18
  599.8 1.1 copy-start
  602.5 0.9 copy-start.1
  603.4 27.2 %all-gather.2.cloned.1.call-start = ((), (), s32[]{:S(2)}) async-start(), calls=%async_computation | async-start | bytes 3538944 | tf_op jit(solution)/shard_map/while/body/eval_jaxpr/all_gather | solution.py:18
  657.8 1.1 copy-start
  660.6 0.9 copy-start.1
  661.4 27.5 %all-gather.2.cloned.1.call-start = ((), (), s32[]{:S(2)}) async-start(), calls=%async_computation | async-start | bytes 3538944 | tf_op jit(solution)/shard_map/while/body/eval_jaxpr/all_gather | solution.py:18
  716.2 1.1 copy-start
  718.9 0.9 copy-start.1
  719.8 27.2 %all-gather.2.cloned.1.call-start = ((), (), s32[]{:S(2)}) async-start(), calls=%async_computation | async-start | bytes 3538944 | tf_op jit(solution)/shard_map/while/body/eval_jaxpr/all_gather | solution.py:18
  774.2 1.1 copy-start
  777.0 0.9 copy-start.1
  777.8 27.5 %all-gather.2.cloned.1.call-start = ((), (), s32[]{:S(2)}) async-start(), calls=%async_computation | async-start | bytes 3538944 | tf_op jit(solution)/shard_map/while/body/eval_jaxpr/all_gather | solution.py:18
  832.6 1.1 copy-start
  835.3 0.9 copy-start.1
  836.2 27.2 %all-gather.2.cloned.1.call-start = ((), (), s32[]{:S(2)}) async-start(), calls=%async_computation | async-start | bytes 3538944 | tf_op jit(solution)/shard_map/while/body/eval_jaxpr/all_gather | solution.py:18
  890.6 1.1 copy-start
  893.4 0.9 copy-start.1
  894.2 27.2 %all-gather.2.cloned.1.call-start = ((), (), s32[]{:S(2)}) async-start(), calls=%async_computation | async-start | bytes 3538944 | tf_op jit(solution)/shard_map/while/body/eval_jaxpr/all_gather | solution.py:18
  948.7 1.1 copy-start
  951.4 0.9 copy-start.1
  952.3 27.2 %all-gather.2.cloned.1.call-start = ((), (), s32[]{:S(2)}) async-start(), calls=%async_computation | async-start | bytes 3538944 | tf_op jit(solution)/shard_map/while/body/eval_jaxpr/all_gather | solution.py:18
  1006.7 1.1 copy-start
  1009.4 0.9 copy-start.1
  1010.3 9.3 copy-start.2
Sparse Core Ops, SparseCore 0:
  77.6 28.9 all-gather.1
  140.4 24.4 all-gather.1
  198.8 24.4 all-gather.1
  256.9 24.4 all-gather.1
  314.9 24.4 all-gather.1
  372.9 24.4 all-gather.1
  431.3 24.4 all-gather.1
  489.7 24.4 all-gather.1
  548.0 24.4 all-gather.1
  606.1 24.4 all-gather.1
  664.4 24.4 all-gather.1
  722.4 24.4 all-gather.1
  780.8 24.4 all-gather.1
  838.9 24.4 all-gather.1
  896.9 24.4 all-gather.1
  954.9 24.4 all-gather.1
where the time goes:
time: 1030 us
  matrix products  548 us (53%)
  waiting for transfers between devices  316 us (31%)
  local copies, waits for them, and re-layouts  102 us (10%)
  other arithmetic  45.6 us (4%)
  between operations  13.7 us (1%)
    dot_general x16, matrix products, step_fn(): jnp.dot(h_gathered, w_rec_flat, preferred_element_type=jnp.float32)  436 us
    all_gather x16, waiting for transfers between devices, step_fn(): lax.all_gather(h_prev.astype(jnp.bfloat16), 'model', axis=1, tiled=True)  315 us
    dot_general x16, matrix products, step_fn(): jnp.dot(x_step, w_in_flat, preferred_element_type=jnp.float32)  112 us
    unnamed x10, local copies, waits for them, and re-layouts  67.4 us
    dynamic_update_slice x16, other arithmetic, local_fn(): lax.scan(step_fn, (h_init, c_init), jnp.swapaxes(x, 0, 1))  25.6 us
    while x64, local copies, waits for them, and re-layouts  24.9 us
  transfers between devices with their start and end apart: 16, of which 16 were waited for; matrix products, arithmetic and copies ran while one was open for 11% of the time, Pallas kernels for 0%

commit v1 on v0

v1 whole, which is shorter than its diff:
```python
import functools

import jax
import jax.numpy as jnp
from jax import lax
from jax.experimental import pallas as pl
from jax.experimental.pallas import tpu as pltpu
from jax.sharding import PartitionSpec as P

CORES = 2
CHUNKS = 4
NSLOT = 3

RIGHT, LEFT, PARTNER, P_RIGHT, P_LEFT, OPPOSITE, P_OPPOSITE = range(7)


def lstm_kernel(n, steps, x_ref, wx_ref, wh_ref, bias_ref, h0_ref, c0_ref,
                y_ref, hl_ref, cl_ref,
                hbuf, wres, wstr, acc, cst, send_sem, recv_sem, res_sem, str_sem, loc_sem, y_sem, x_sem):
    rows, half = hbuf.shape[1], hbuf.shape[2]
    units = 2 * half
    piece = units // CHUNKS
    chips = n // CORES
    nblk = n + 1
    me = lax.axis_index("model")
    chip, core = me // CORES, me % CORES
    other = 1 - core
    right_chip, left_chip = (chip + 1) % chips, (chip + chips - 1) % chips
    far_chip = (chip + 2) % chips
    own = chip * CORES + core
    partner = chip * CORES + other
    right = right_chip * CORES + core
    left = left_chip * CORES + core
    p_right = right_chip * CORES + other
    p_left = left_chip * CORES + other
    far = far_chip * CORES + core
    p_far = far_chip * CORES + other

    passes = [
        ((None, 0), (None, 1)),
        ((own, 0), (own, 1)),
        ((partner, 0), (partner, 1)),
        ((right, 0), (left, 0)),
        ((right, 1), (left, 1)),
        ((p_right, 0), (p_left, 0)),
        ((p_right, 1), (p_left, 1)),
        ((far, 0), (far, 1)),
        ((p_far, 0), (p_far, 1)),
    ]
    npass = len(passes)

    def weight_src(part):
        blk, hf = part
        if blk is None:
            return wx_ref.at[pl.ds(hf * half, half)]
        return wh_ref.at[pl.ds(pl.multiple_of(blk * units + hf * half, half), half)]

    def hidx(slot, blk, hf):
        return (slot * nblk + (n if blk is None else blk)) * 2 + hf

    def resident(j):
        return pltpu.make_async_copy(weight_src(passes[j][0]), wres.at[j], res_sem.at[j])

    def streamed(j):
        return pltpu.make_async_copy(weight_src(passes[j][1]), wstr.at[j % NSLOT], str_sem.at[j % NSLOT])

    def x_copies(t, slot):
        return [
            pltpu.make_async_copy(x_ref.at[t, :, pl.ds(hf * half, half)], hbuf.at[hidx(slot, None, hf)], x_sem.at[hf])
            for hf in range(2)
        ]

    def y_copies(t, slot):
        return [
            pltpu.make_async_copy(hbuf.at[hidx(slot, own, hf)], y_ref.at[t, :, pl.ds(hf * half, half)], y_sem.at[hf])
            for hf in range(2)
        ]

    def remote(kind, c, slot):
        src_blk = {RIGHT: own, LEFT: own, PARTNER: own, P_RIGHT: right, P_LEFT: left,
                   OPPOSITE: right if c % 2 == 0 else left, P_OPPOSITE: far}[kind]
        dst = {RIGHT: left, LEFT: right, PARTNER: partner, P_RIGHT: partner, P_LEFT: partner,
               OPPOSITE: left if c % 2 == 0 else right, P_OPPOSITE: partner}[kind]
        view = hbuf.at[hidx(slot, src_blk, c // 2), :, pl.ds((c % 2) * piece, piece)]
        return pltpu.make_async_remote_copy(
            src_ref=view, dst_ref=view, send_sem=send_sem.at[kind, c], recv_sem=recv_sem.at[slot, kind, c],
            device_id={"model": dst}, device_id_type=pl.DeviceIdType.MESH)

    def arrive(kind, c, slot):
        blk = {RIGHT: right, LEFT: left, PARTNER: partner, P_RIGHT: p_right, P_LEFT: p_left,
               OPPOSITE: far, P_OPPOSITE: p_far}[kind]
        view = hbuf.at[hidx(slot, blk, c // 2), :, pl.ds((c % 2) * piece, piece)]
        pltpu.make_async_remote_copy(
            src_ref=view, dst_ref=view, send_sem=send_sem.at[kind, c], recv_sem=recv_sem.at[slot, kind, c],
            device_id={"model": partner}, device_id_type=pl.DeviceIdType.MESH).wait_recv()

    def send_own(c, slot):
        for kind in (RIGHT, LEFT, PARTNER):
            remote(kind, c, slot).start()

    def pass_on(c, slot):
        arrive(RIGHT, c, slot)
        if c % 2 == 0:
            remote(OPPOSITE, c, slot).start()
        remote(P_RIGHT, c, slot).start()
        arrive(LEFT, c, slot)
        if c % 2 == 1:
            remote(OPPOSITE, c, slot).start()
        remote(P_LEFT, c, slot).start()

    def sends_done(slot):
        for kind in range(7):
            for c in range(CHUNKS):
                remote(kind, c, slot).wait_send()

    h0_copy = pltpu.make_async_copy(h0_ref, acc.at[:, pl.ds(0, units)], loc_sem.at[0])
    c0_copy = pltpu.make_async_copy(c0_ref, cst, loc_sem.at[1])
    h0_copy.start()
    c0_copy.start()
    for cp in x_copies(0, 0):
        cp.start()
    for j in range(npass):
        resident(j).start()
        if j < NSLOT:
            streamed(j).start()

    barrier = pltpu.get_barrier_semaphore()
    for peer in (left, right, partner):
        pl.semaphore_signal(barrier, inc=1, device_id={"model": peer}, device_id_type=pl.DeviceIdType.MESH)
    pl.semaphore_wait(barrier, 3)

    h0_copy.wait()
    for hf in range(2):
        hbuf[hidx(0, own, hf)] = acc[:, hf * half:(hf + 1) * half].astype(jnp.bfloat16)
    for c in range(CHUNKS):
        send_own(c, 0)
    c0_copy.wait()

    def accumulate(j, slot):
        (ba, ha), (bb, hb) = passes[j]
        ia, ib = hidx(slot, ba, ha), hidx(slot, bb, hb)
        ntile = half
        for k in range(4 * units // ntile):
            cols = slice(k * ntile, (k + 1) * ntile)
            add = jnp.dot(hbuf[ia], wres[j, :, cols], preferred_element_type=jnp.float32)
            add += jnp.dot(hbuf[ib], wstr[j % NSLOT, :, cols], preferred_element_type=jnp.float32)
            if j == 0:
                acc[:, cols] = add + bias_ref[:, cols]
            else:
                acc[:, cols] += add

    def finish(c, slot, nxt):
        parts = []
        for j in (npass - 2, npass - 1):
            (ba, ha), (bb, hb) = passes[j]
            parts.append((hidx(slot, ba, ha), wres, j))
            parts.append((hidx(slot, bb, hb), wstr, j % NSLOT))
        for g in range(4):
            cols = slice(g * units + c * piece, g * units + (c + 1) * piece)
            add = None
            for ih, wref, jw in parts:
                term = jnp.dot(hbuf[ih], wref[jw, :, cols], preferred_element_type=jnp.float32)
                add = term if add is None else add + term
            acc[:, cols] += add
        own_idx = hidx(nxt, own, c // 2)
        rblk = 16
        for r in range(rows // rblk):
            rs = slice(r * rblk, (r + 1) * rblk)
            us = slice(c * piece, (c + 1) * piece)
            gi, gf, go, gu = (acc[rs, g * units + c * piece:g * units + (c + 1) * piece] for g in range(4))
            si = 0.5 * jnp.tanh(0.5 * gi) + 0.5
            sf = 0.5 * jnp.tanh(0.5 * gf) + 0.5
            so = 0.5 * jnp.tanh(0.5 * go) + 0.5
            cn = sf * cst[rs, us] + si * jnp.tanh(gu)
            hn = so * jnp.tanh(cn)
            cst[rs, us] = cn
            acc[rs, us] = hn
            hbuf[own_idx, rs, (c % 2) * piece:(c % 2 + 1) * piece] = hn.astype(jnp.bfloat16)

    def step(t, carry):
        slot = t % 2
        nxt = 1 - slot
        first, last = t == 0, t == steps - 1

        def weights(j):
            @pl.when(first)
            def _():
                resident(j).wait()
            streamed(j).wait()

        def refill(j):
            k = j + NSLOT
            if k < npass:
                streamed(k).start()
            else:
                @pl.when(jnp.logical_not(last))
                def _():
                    streamed(k - npass).start()

        for cp in x_copies(t, slot):
            cp.wait()
        weights(0)
        accumulate(0, slot)
        refill(0)
        weights(1)
        accumulate(1, slot)
        refill(1)
        pass_on(0, slot)
        pass_on(1, slot)
        for c in range(CHUNKS):
            arrive(PARTNER, c, slot)
        weights(2)
        accumulate(2, slot)
        refill(2)
        pass_on(2, slot)
        weights(3)
        accumulate(3, slot)
        refill(3)
        pass_on(3, slot)
        weights(4)
        accumulate(4, slot)
        refill(4)
        for c in range(2):
            arrive(P_RIGHT, c, slot)
            arrive(P_LEFT, c, slot)
        weights(5)
        accumulate(5, slot)
        refill(5)
        for c in range(CHUNKS):
            arrive(OPPOSITE, c, slot)
            remote(P_OPPOSITE, c, slot).start()
        for c in range(2, CHUNKS):
            arrive(P_RIGHT, c, slot)
            arrive(P_LEFT, c, slot)
        weights(6)
        accumulate(6, slot)
        refill(6)
        weights(7)
        weights(8)
        for c in range(CHUNKS):
            arrive(P_OPPOSITE, c, slot)
        sends_done(slot)

        @pl.when(jnp.logical_not(first))
        def _():
            for cp in y_copies(t - 1, slot):
                cp.wait()

        @pl.when(jnp.logical_not(last))
        def _():
            for cp in x_copies(t + 1, nxt):
                cp.start()

        for c in range(CHUNKS):
            finish(c, slot, nxt)

            @pl.when(jnp.logical_not(last))
            def _():
                send_own(c, nxt)
        refill(7)
        refill(8)
        for cp in y_copies(t, nxt):
            cp.start()
        return carry

    lax.fori_loop(0, steps, step, 0)
    end = steps % 2
    hl_copy = pltpu.make_async_copy(acc.at[:, pl.ds(0, units)], hl_ref, loc_sem.at[0])
    cl_copy = pltpu.make_async_copy(cst, cl_ref, loc_sem.at[1])
    hl_copy.start()
    cl_copy.start()
    for cp in y_copies(steps - 1, end):
        cp.wait()
    hl_copy.wait()
    cl_copy.wait()


def solution(mesh):
    n = mesh.shape["model"]

    def local_fn(x, w_in, w_rec, gate_bias, h_init, c_init):
        in_dim, hidden = w_in.shape[0], w_rec.shape[0]
        units = w_rec.shape[2]
        rows, steps = x.shape[0], x.shape[1]
        half = units // 2
        assert in_dim == units and n == 8
        anyspec = pl.BlockSpec(memory_space=pl.ANY)
        dma = pltpu.SemaphoreType.DMA
        y, h_last, c_last = pl.pallas_call(
            functools.partial(lstm_kernel, n, steps),
            name="lstm",
            out_shape=(
                jax.ShapeDtypeStruct((steps, rows, units), jnp.bfloat16),
                jax.ShapeDtypeStruct((rows, units), jnp.float32),
                jax.ShapeDtypeStruct((rows, units), jnp.float32),
            ),
            in_specs=[anyspec, anyspec, anyspec, pl.BlockSpec(memory_space=pltpu.VMEM), anyspec, anyspec],
            out_specs=(anyspec, anyspec, anyspec),
            scratch_shapes=[
                pltpu.VMEM((2 * (n + 1) * 2, rows, half), jnp.bfloat16),
                pltpu.VMEM((n + 1, half, 4 * units), jnp.bfloat16),
                pltpu.VMEM((NSLOT, half, 4 * units), jnp.bfloat16),
                pltpu.VMEM((rows, 4 * units), jnp.float32),
                pltpu.VMEM((rows, units), jnp.float32),
                dma((7, CHUNKS)),
                dma((2, 7, CHUNKS)),
                dma((n + 1,)),
                dma((NSLOT,)),
                dma((2,)),
                dma((2,)),
                dma((2,)),
            ],
            compiler_params=pltpu.CompilerParams(
                collective_id=0, has_side_effects=True, vmem_limit_bytes=67043328),
        )(jnp.swapaxes(x, 0, 1), w_in.reshape(in_dim, 4 * units), w_rec.reshape(hidden, 4 * units),
          gate_bias.reshape(1, 4 * units), h_init, c_init)
        return jnp.swapaxes(y, 0, 1), h_last, c_last

    return jax.shard_map(
        local_fn,
        mesh=mesh,
        in_specs=(P("data", None, None), P(None, None, "model"), P(None, None, "model"),
                  P(None, "model"), P("data", "model"), P("data", "model")),
        out_specs=(P("data", None, "model"), P("data", "model"), P("data", "model")),
        check_vma=False,
    )
```

time: 1030 us -> 434 us (0.42)
  matrix products: 548 us -> 0 us
  Pallas kernels: 0 us -> 356 us
  waiting for transfers between devices: 316 us -> 0 us
  other arithmetic: 45.6 us -> 0 us
  local copies, waits for them, and re-layouts: 102 us -> 77.4 us
  between operations: 13.7 us -> 0.66 us
    dot_general x32 -> x0, matrix products: 548 us -> none  [the longest x16 436 us: step_fn(): jnp.dot(h_gathered, w_rec_flat, preferred_element_type=jnp.float32)]
    pallas_call x0 -> x1, Pallas kernels: none -> 356 us  [local_fn(): pl.pallas_call(functools.partial(lstm_kernel, n, steps), name='lstm', out...]
    all_gather x16 -> x0, waiting for transfers between devices: 315 us -> none  [step_fn(): lax.all_gather(h_prev.astype(jnp.bfloat16), 'model', axis=1, tiled=True)]
    while x65 -> x0, local copies, waits for them, and re-layouts: 34.2 us -> none
    dynamic_update_slice x16 -> x0, other arithmetic: 25.6 us -> none  [local_fn(): lax.scan(step_fn, (h_init, c_init), jnp.swapaxes(x, 0, 1))]
    convert_element_type x16 -> x0, other arithmetic: 12.9 us -> none  [step_fn(): h_prev.astype(jnp.bfloat16)]
    unnamed x10 -> x11, local copies, waits for them, and re-layouts: 67.4 us -> 77.4 us
  transfers between devices with their start and end apart: 16 -> 0, of which waited for: 16 -> 0; matrix products, arithmetic and copies ran while one was open for 11% -> 0% of each run, Pallas kernels for 0% -> 0%
where the time goes in v1:
time: 434 us
  Pallas kernels  356 us (82%)
  local copies, waits for them, and re-layouts  77.4 us (18%)
    pallas_call x1, Pallas kernels, local_fn(): pl.pallas_call(functools.partial(lstm_kernel, n, steps), name='lstm', out...  356 us
    unnamed x11, local copies, waits for them, and re-layouts  77.4 us

profile of v1, /device:TPU:81, one launch (start us, length us, event | category | flops | bytes accessed | tf_op | source)
XLA Modules:
  0.0 433.6 jit_solution(15882425820377162386)
XLA Ops:
  0.6 1.3 copy.13
  2.0 9.0 %copy.15 = bf16[192,16,1024]{2,0,1:T(8,128)(2,1)} copy(bf16[192,16,1024]{2,1,0:T(8,128)(2,1)} %param.6) | data formatting | bytes 12582912 | tf_op args[0]
  11.0 12.1 %copy.11 = bf16[128,8,4,1024]{3,1,2,0:T(8,128)(2,1)} copy(bf16[128,8,4,1024]{3,2,1,0:T(4,128)(2,1)} %bitcast.13) | data formatting | bytes 16777216
  23.0 44.1 %copy.12 = bf16[1024,8,4,1024]{3,1,2,0:T(8,128)(2,1)} copy(bf16[1024,8,4,1024]{3,2,1,0:T(4,128)(2,1)} %bitcast.4) | data formatting | bytes 134217728
  67.2 355.5 %lstm.1 = (bf16[16,192,1024]{2,1,0:T(8,128)(2,1)}, f32[192,1024]{1,0:T(8,128)}, f32[192,1024]{1,0:T(8,128)}) custom-call(bf16[16,192,1024]{2,1,0:T(8,128)(2,1)} %bitcast.12, bf16[1024,4096]{1,0:T(8,128)(2,1)} %bitcast.11, bf16[8192,4096]{1,0:T(8,128)(2,1)} %bitcast.5.wh_ref, f32[1,4096]{1,0:T(1,128)} %bitcast.15, f32[192,1024]{1,0:T(8,128)} %h0_ref.1, ...), custom_call_target="tpu_custom_call" | custom-call | tf_op jit(solution)/shard_map/lstm/pallas_call | solution.py:289
  422.7 0.0 copy-start.1
  422.7 0.0 copy-start
  422.7 9.1 %copy.10 = bf16[192,16,1024]{2,1,0:T(8,128)(2,1)} copy(bf16[192,16,1024]{2,0,1:T(8,128)(2,1)} %bitcast.14) | data formatting | bytes 12582912
  431.9 0.0 copy-done.1
  431.9 0.9 copy.18
  432.7 0.0 copy-done
  432.7 0.9 copy.19
Async XLA Ops:
  422.7 9.1 %copy-start.1 = (f32[192,1024]{1,0:T(8,128)S(1)}, f32[192,1024]{1,0:T(8,128)}, u32[]{:S(2)}) copy-start(f32[192,1024]{1,0:T(8,128)} %get-tuple-element.16) | copy-start | bytes 2359300
  422.7 10.0 %copy-start = (f32[192,1024]{1,0:T(8,128)S(1)}, f32[192,1024]{1,0:T(8,128)}, u32[]{:S(2)}) copy-start(f32[192,1024]{1,0:T(8,128)} %get-tuple-element.17) | copy-start | bytes 2359300
